TPU v7x, 32 devices: a whole 2x2x4 slice. The times are simulated.
32 devices in a mesh: job: 2 (over y), ta: 4 (over z), xyz: 2 (over x), src: 2 (over core).
Axes of the slice: x: 2, y: 2, z: 4, core: 2. Of those that a mesh axis runs over, the one named last changes fastest.
Arguments:
- spinors: float32 [64, 8, 2, 8, 3, 512], P('src', 'ta', None, 'job', None, 'xyz'), parts along dimension 3, may hold values from -6 to 6
- eigvecs: float32 [8, 256, 2, 3, 512], P('ta', 'job', None, None, 'xyz'), parts along dimension 1, may hold values from -0.109375 to 0.109375
- group_of: int32 [8], replicated, may hold values from 0 to 3, as said below
- source_ids: int32 [64], P('src'), may hold values from 0 to 63, as said below
Outputs:
- perambulator: float32 [8, 2, 8, 64, 128], P('ta', None, 'job', 'src', 'xyz'), parts along dimension 2
There are 2 independent parts, one for each index of `job`. A program takes and returns all parts, laid end to end along the dimension named above; an argument that names none is the same for every part. Nothing has to cross between parts.
Inputs may be any that keep to these rules, and one draw needn't show every extreme that they name: `group_of`: every group number appears exactly 2 times. `source_ids`: the 32 entries held by index i of src are a permutation of i * 32 to (i + 1) * 32 - 1.
All inputs are finite; a program needn't handle non-finite values.
Results may differ from a plain program's by a relative error of at most 0.00007.
Values sent between devices are 32-bit elements; how exact they have to be, the bound alone decides.
A program may use at most 64 MiB of HBM per device.

v0:
```python
import functools

import jax
import jax.numpy as jnp
from jax import lax
from jax.experimental import pallas as pl
from jax.experimental.pallas import tpu as pltpu
from jax.sharding import PartitionSpec as P

MESH = pl.DeviceIdType.MESH
OUT_PIECES = 4
PIECE_LAYERS = 1
LANES = 128
SUBLANES = 8


def contract_pair(vectors, spinor):
    vector_real = vectors[:, :, 0]
    vector_imag = vectors[:, :, 1]
    spinor_real = spinor[:, :, 0]
    spinor_imag = spinor[:, :, 1]

    def contract(left_side, right_side):
        return jnp.einsum(
            "tkcx,ntscx->tsnk", left_side, right_side, precision=lax.Precision.HIGHEST
        )

    real_part = contract(vector_real, spinor_real) + contract(vector_imag, spinor_imag)
    imag_part = contract(vector_real, spinor_imag) - contract(vector_imag, spinor_real)
    return jnp.stack([real_part, imag_part], axis=1)


def local_general(spinors, eigvecs, group_of, source_ids):
    extent = group_of.shape[0]
    sort_keys = group_of * extent + jnp.arange(extent, dtype=jnp.int32)
    ordering = jnp.argsort(sort_keys)
    spread = lax.all_to_all(spinors, "ta", split_axis=0, concat_axis=1, tiled=True)
    grouped = jnp.take(spread, ordering, axis=1)
    regrouped = lax.all_to_all(grouped, "ta", split_axis=1, concat_axis=0, tiled=True)
    partial_sums = contract_pair(eigvecs, regrouped)
    summed = lax.psum_scatter(partial_sums, "xyz", scatter_dimension=4, tiled=True)
    inverse = jnp.argsort(source_ids)
    return jnp.take(summed, inverse, axis=3)


def copy_to(src, dst, sems, index, where):
    return pltpu.make_async_remote_copy(
        src_ref=src,
        dst_ref=dst,
        send_sem=sems.at[0, index],
        recv_sem=sems.at[1, index],
        device_id=where,
        device_id_type=MESH,
    )


def routes(words, which, wanted, goes_to, right, m, spots):
    extent = len(wanted)
    half = extent // 2
    crosses, slot = [], []
    for item in range(extent):
        over = goes_to[item] >= half if item < half else goes_to[item] < half
        crosses.append(jnp.where(over, 1, 0))
        slot.append(sum(crosses[item // half * half:item], jnp.int32(0)))
        words[which, 0, item] = wanted[item]
        words[which, 1, item] = slot[item]
    mine = [jnp.where(right == 1, crosses[half + i], crosses[i]) for i in range(half)]
    mine_slot = [jnp.where(right == 1, slot[half + i], slot[i]) for i in range(half)]
    send = []
    for place in range(m):
        at = jnp.int32(0)
        for i in range(half):
            at = at + jnp.where(mine_slot[i] == place, i * mine[i], 0)
        send.append(at)

    def pick(q):
        want = words[which, 0, right * half + q]
        own = jnp.where(want >= half, 1, 0) == right
        near = jnp.where(own, want - right * half, 0)
        far = jnp.where(own, 0, words[which, 1, want])
        return near, jnp.minimum(far, m - 1), own

    return send, [[pick(q) for q in group] for group in spots]


def sites_apart(value):
    pairs = value.reshape(value.shape[0] // 2, 2, SUBLANES, LANES)
    even, odd = pairs[:, 0], pairs[:, 1]
    upper = lax.broadcasted_iota(jnp.int32, even.shape, 1) < SUBLANES // 2
    shift = SUBLANES // 2
    first = jnp.where(upper, even, pltpu.roll(odd, shift, 1))
    second = jnp.where(upper, pltpu.roll(even, shift, 1), odd)
    return first.reshape(-1, LANES), second.reshape(-1, LANES)


def kernel(n, m, plan, group_ref, e_ref, s_ref, out_ref, *scratch):
    held = e_ref.shape[0]
    pieces = len(plan)
    scratch = list(scratch)

    def take(count):
        got = scratch[:count]
        del scratch[:count]
        return got

    side_e, mid_e, recv_e, give_e = take(pieces), take(pieces), take(pieces), take(pieces)
    side_o, mid_o, recv_o, give_o = (
        take(OUT_PIECES), take(OUT_PIECES), take(OUT_PIECES), take(OUT_PIECES)
    )
    full, high, low, acc, x_recv, o_recv, o_send, spin_raw, words = take(9)
    in_e, cross_e, back_e, core_e, x_sem, in_o, cross_o, back_o, s_sem = take(9)

    load_s = pltpu.make_async_copy(s_ref, spin_raw, s_sem)
    load_s.start()

    z = lax.axis_index("ta")
    core = lax.axis_index("src")
    xi = lax.axis_index("xyz")
    right = z // (n // 2)
    inner = jnp.logical_and(z > 0, z < n - 1)
    outer = jnp.logical_not(inner)
    to_inner = {"ta": 1 + right}
    to_outer = {"ta": right * (n - 1)}
    to_other = {"ta": n - 1 - z}
    to_core = {"src": 1 - core}
    to_x = {"xyz": 1 - xi}
    outer_at = right * held
    own_at = (1 - right) * held
    depth = e_ref.shape[2] // 2

    def rows_at(who, i):
        first, count = plan[i]
        at = pl.multiple_of(who * depth, depth)
        return slice(None), pl.ds(first, count), pl.ds(at, depth), slice(None)

    def mine_at(i):
        return rows_at(core, i)

    barrier = pltpu.get_barrier_semaphore()
    for where in (to_core, to_x):
        pl.semaphore_signal(barrier, inc=1, device_id=where, device_id_type=MESH)

    @pl.when(inner)
    def _():
        for where in (to_outer, to_other):
            pl.semaphore_signal(barrier, inc=1, device_id=where, device_id_type=MESH)
        pl.semaphore_wait(barrier, 4)

    @pl.when(outer)
    def _():
        pl.semaphore_signal(barrier, inc=1, device_id=to_inner, device_id_type=MESH)
        pl.semaphore_wait(barrier, 3)

    def inward_e(i):
        return copy_to(
            e_ref.at[mine_at(i)], side_e[i].at[pl.ds(outer_at, held)], in_e, i, to_inner
        )

    def across_e(i):
        return copy_to(mid_e[i], recv_e[i], cross_e, i, to_other)

    def back_out_e(i):
        return copy_to(give_e[i], full.at[rows_at(core, i)], back_e, i, to_outer)

    def swap_e(i):
        view = full.at[rows_at(core, i)]
        return copy_to(view, view, core_e, i, to_core)

    def swapped_e(i):
        view = full.at[rows_at(1 - core, i)]
        return copy_to(view, view, core_e, i, to_core)

    def chosen(pick, side, recv):
        near, far, own = pick
        return jnp.where(own, side[near], recv[far])

    @pl.when(outer)
    def _():
        for j in range(pieces):
            inward_e(j).start()

    @pl.when(inner)
    def _():
        for j in range(pieces):
            side_e[j][pl.ds(own_at, held)] = e_ref[mine_at(j)]

    extent = n * held
    group = [group_ref[t] for t in range(extent)]
    rank, ordering = [], []
    for t in range(extent):
        before = sum((jnp.where(group[u] == group[t], 1, 0) for u in range(t)), jnp.int32(0))
        rank.append(group[t] * held + before)
    for r in range(extent):
        ordering.append(
            sum((jnp.where(rank[t] == r, t, 0) for t in range(extent)), jnp.int32(0))
        )
    spots = [[outer_at + i for i in range(held)], [own_at + i for i in range(held)]]
    send_e, (outer_e, own_e) = routes(words, 0, rank, ordering, right, m, spots)
    send_o, (outer_o, own_o) = routes(words, 1, ordering, rank, right, m, spots)

    def split(value):
        top = value.astype(jnp.bfloat16)
        return top, (value - top.astype(jnp.float32)).astype(jnp.bfloat16)

    load_s.wait()
    width = acc.shape[2] // 2
    for t in range(held):
        acc[t] = jnp.zeros(acc.shape[1:], jnp.float32)
        for c in range(high.shape[1] // 2):
            reals = sites_apart(spin_raw[:, t, 0, c])
            imags = sites_apart(spin_raw[:, t, 1, c])
            for tile, (real_, imag_) in enumerate(zip(reals, imags)):
                at = slice(tile * LANES, (tile + 1) * LANES)
                for keep, real, imag in zip((high, low), split(real_), split(imag_)):
                    keep[t, 2 * c, :width, at] = real
                    keep[t, 2 * c, width:, at] = imag
                    keep[t, 2 * c + 1, :width, at] = imag
                    keep[t, 2 * c + 1, width:, at] = -real

    def dot(a, b):
        return lax.dot_general(
            a, b, (((1,), (1,)), ((), ())), preferred_element_type=jnp.float32
        )

    def contract(j):
        for t in range(held):
            top, rest = split(full[t, j])
            acc[t] += dot(top, high[t, j]) + (dot(top, low[t, j]) + dot(rest, high[t, j]))

    for tick in range(pieces + 3):
        i, before, late = tick, tick - 1, tick - 2

        @pl.when(inner)
        def _():
            if i < pieces:
                inward_e(i).wait_recv()
                for slot in range(m):
                    mid_e[i][slot] = side_e[i][send_e[slot]]
                across_e(i).start()
            if 0 <= before < pieces:
                across_e(before).wait_recv()
                for k in range(held):
                    give_e[before][k] = chosen(outer_e[k], side_e[before], recv_e[before])
                back_out_e(before).start()
                _, layers_, rows_, _ = rows_at(core, before)
                for k in range(held):
                    full[k, layers_, rows_, :] = chosen(own_e[k], side_e[before], recv_e[before])
                swap_e(before).start()

        if 0 <= late < pieces:
            @pl.when(outer)
            def _():
                back_out_e(late).wait_recv()
                swap_e(late).start()

        last = tick - 3
        if last >= 0:
            swapped_e(last).wait_recv()
            for layer in range(plan[last][0], sum(plan[last])):
                contract(layer)

    for i in range(pieces):
        swap_e(i).wait_send()

    @pl.when(inner)
    def _():
        for i in range(pieces):
            across_e(i).wait_send()
            back_out_e(i).wait_send()

    @pl.when(outer)
    def _():
        for i in range(pieces):
            inward_e(i).wait_send()

    rows = acc.shape[1] // 2
    part = rows // OUT_PIECES

    def x_swap(q):
        there = pl.ds(pl.multiple_of((1 - xi) * rows + q * part, part), part)
        return copy_to(acc.at[:, there, :], x_recv.at[q], x_sem, q, to_x)

    def summed(q):
        here = pl.ds(pl.multiple_of(xi * rows + q * part, part), part)
        return acc[:, here, :] + x_recv[q]

    def inward_o(q):
        return copy_to(o_send.at[q], side_o[q].at[pl.ds(outer_at, held)], in_o, q, to_inner)

    def across_o(q):
        return copy_to(mid_o[q], recv_o[q], cross_o, q, to_other)

    def back_out_o(q):
        return copy_to(give_o[q], o_recv.at[q], back_o, q, to_outer)

    for q in range(OUT_PIECES):
        x_swap(q).start()

    @pl.when(outer)
    def _():
        for q in range(OUT_PIECES):
            x_swap(q).wait_recv()
            o_send[q] = summed(q)
            inward_o(q).start()
        for q in range(OUT_PIECES):
            back_out_o(q).wait_recv()
            out_ref[:, q * part:(q + 1) * part, :] = o_recv[q]
        for q in range(OUT_PIECES):
            inward_o(q).wait_send()

    @pl.when(inner)
    def _():
        for q in range(OUT_PIECES):
            x_swap(q).wait_recv()
            side_o[q][pl.ds(own_at, held)] = summed(q)
        for q in range(OUT_PIECES):
            inward_o(q).wait_recv()
            for slot in range(m):
                mid_o[q][slot] = side_o[q][send_o[slot]]
            across_o(q).start()
        for q in range(OUT_PIECES):
            across_o(q).wait_recv()
            for i in range(held):
                give_o[q][i] = chosen(outer_o[i], side_o[q], recv_o[q])
            back_out_o(q).start()
            for i in range(held):
                out_ref[i, q * part:(q + 1) * part, :] = chosen(own_o[i], side_o[q], recv_o[q])
        for q in range(OUT_PIECES):
            across_o(q).wait_send()
            back_out_o(q).wait_send()

    for q in range(OUT_PIECES):
        x_swap(q).wait_send()


def local_line(n, spinors, eigvecs, group_of, source_ids):
    extent = group_of.shape[0]
    half = extent // 2
    sources, held, _, spins, colours, sites = spinors.shape
    vectors = eigvecs.shape[1]
    layers = 2 * colours
    plan = [
        (first, min(PIECE_LAYERS, layers - first)) for first in range(0, layers, PIECE_LAYERS)
    ]
    depth = vectors // 2
    width = spins * sources

    count = jnp.sum((group_of[:half] >= n // 2).astype(jnp.int32))

    e_view = eigvecs.transpose(0, 3, 2, 1, 4).reshape(held, layers, vectors, sites)
    tiled = spinors.reshape(sources, held, 2, spins, colours, sites // LANES, LANES)
    s_view = tiled.transpose(0, 1, 2, 4, 5, 3, 6).reshape(
        sources, held, 2, colours, SUBLANES, LANES
    )

    rows = vectors // 2
    part = rows // OUT_PIECES
    f32 = jnp.float32

    def run(m):
        vmem = pl.BlockSpec(memory_space=pltpu.VMEM)
        e_items = [(size, depth, sites) for _, size in plan]
        o_item = (part, 2 * width)
        buffers = []
        for pieces_ in (e_items, [o_item] * OUT_PIECES):
            for slots in (half, m, m, held):
                buffers += [pltpu.VMEM((slots,) + item, f32) for item in pieces_]
        return pl.pallas_call(
            functools.partial(kernel, n, m, plan),
            name=f"project_{m}",
            out_shape=jax.ShapeDtypeStruct((held, rows, 2 * width), f32),
            in_specs=[
                pl.BlockSpec(memory_space=pltpu.SMEM), vmem, pl.BlockSpec(memory_space=pl.ANY)
            ],
            out_specs=vmem,
            scratch_shapes=buffers + [
                pltpu.VMEM((held, layers, vectors, sites), f32),
                pltpu.VMEM((held, layers, 2 * width, sites), jnp.bfloat16),
                pltpu.VMEM((held, layers, 2 * width, sites), jnp.bfloat16),
                pltpu.VMEM((held, vectors, 2 * width), f32),
                pltpu.VMEM((OUT_PIECES, held) + o_item, f32),
                pltpu.VMEM((OUT_PIECES, held) + o_item, f32),
                pltpu.VMEM((OUT_PIECES, held) + o_item, f32),
                pltpu.VMEM(s_view.shape, f32),
                pltpu.SMEM((2, 2, extent), jnp.int32),
            ] + [pltpu.SemaphoreType.DMA((2, len(plan)))] * 4
            + [pltpu.SemaphoreType.DMA((2, OUT_PIECES))] * 4 + [pltpu.SemaphoreType.DMA],
            compiler_params=pltpu.CompilerParams(
                collective_id=m, has_side_effects=True, vmem_limit_bytes=48 * 1024 * 1024
            ),
        )

    branches = [run(m) for m in range(1, half + 1)]
    projected = lax.switch(jnp.maximum(count, 1) - 1, branches, group_of, e_view, s_view)
    projected = projected.reshape(held, rows, 2, sources, spins)
    first = lax.axis_index("src") * sources
    place = (source_ids[None, :] - first) == jnp.arange(sources, dtype=jnp.int32)[:, None]
    return jnp.einsum(
        "jn,rkpns->rpsjk", place.astype(f32), projected, precision=lax.Precision.HIGHEST
    )


def solution(mesh):
    in_specs = (
        P("src", "ta", None, "job", None, "xyz"),
        P("ta", "job", None, None, "xyz"),
        P(),
        P("src"),
    )
    out_specs = P("ta", None, "job", "src", "xyz")
    n = mesh.shape["ta"]
    line = n == 4 and mesh.shape["src"] == 2 and mesh.shape["xyz"] == 2

    def local(spinors, eigvecs, group_of, source_ids):
        tiles = spinors.shape[5] // LANES
        if line and tiles == 2 and tiles * spinors.shape[3] == SUBLANES:
            return local_line(n, spinors, eigvecs, group_of, source_ids)
        return local_general(spinors, eigvecs, group_of, source_ids)

    return jax.shard_map(local, mesh=mesh, in_specs=in_specs, out_specs=out_specs, check_vma=False)
```

profile of v0, /device:TPU:0, one launch (start us, length us, event | category | flops | bytes accessed | tf_op | source)
XLA Modules:
  0.0 52.4 jit_solution(17276454912975526427)
XLA Ops:
  0.0 0.0 copy-start.1
  0.0 0.0 copy-start
  0.0 1.7 %copy.12 = f32[2,3,2,128,256]{4,3,2,1,0:T(8,128)S(1)} copy(f32[2,3,2,128,256]{4,2,1,3,0:T(2,128)} %bitcast.27) | data formatting | bytes 3145728 | tf_op jit(solution)/shard_map/transpose | solution.py:350
  1.7 0.0 copy-done.1
  1.7 0.6 %fusion.3 = s32[]{:T(128)} fusion(s32[8]{0:T(128)S(1)} %copy-done.1), kind=kLoop, calls=%fused_computation.5 | loop fusion | flops 11 | bytes 20 | tf_op jit(solution)/shard_map/reduce_sum | solution.py:348
  3.0 0.0 copy-done
  3.0 0.0 copy-start.2
  3.0 48.4 %conditional.1 = (f32[2,64,2,32,4]{1,3,4,2,0:T(8,128)S(1)}) conditional(s32[]{:T(128)} %clamp.3, (s32[8]{0:T(128)S(1)}, f32[2,6,128,256]{3,2,1,0:T(8,128)S(1)}, f32[32,2,2,3,8,128]{5,4,3,2,1,0:T(8,128)S(1)}) %tuple.38, (s32[8]{0:T(128)S(1)}, f32[2,6,128,256]{3,2,1,0:T(8,128)S(1)}, ...), branch_computations={%region_1.0_spmd, %region_2.0_spmd, %region_3.0_spmd, %region_4.0_... | conditional | bytes 524296 | solution.py:394
  3.0 48.2 %project_2.1 = f32[2,64,256]{2,1,0:T(8,128)S(1)} custom-call(s32[8]{0:T(128)S(1)} %get-tuple-element.38.group_ref, f32[2,6,128,256]{3,2,1,0:T(8,128)S(1)} %get-tuple-element.39.e_ref, f32[32,2,2,3,8,128]{5,4,3,2,1,0:T(8,128)S(1)} %get-tuple-element.40.s_ref), custom_call_target="tpu_custom_call" | custom-call | tf_op jit(solution)/shard_map/cond/branch_1_fun/project_2/pallas_call | solution.py:394
  51.3 0.1 copy.9
  51.4 0.0 copy-done.2
  51.5 1.0 %convolution_bitcast_fusion = f32[2,2,4,32,64]{4,3,2,1,0:T(8,128)} fusion(f32[2,64,2,32,4]{1,3,4,2,0:T(8,128)S(1)} %get-tuple-element.47, s32[32]{0:T(128)S(1)} %broadcast_subtract_fusion), kind=kOutput, calls=%fused_computation | convolution fusion | flops 12583936 | bytes 262272 | tf_op jit(solution)/shard_map/jn,rkpns->rpsjk/dot_general | solution.py:398
  (2 shorter events, 0.0 us)
Async XLA Ops:
  0.0 1.7 %copy-start.1 = (s32[8]{0:T(128)S(1)}, s32[8]{0:T(128)}, u32[]{:S(2)}) copy-start(s32[8]{0:T(128)} %param.10) | copy-start | bytes 100
  0.0 3.0 %copy-start = (f32[32,2,2,4,3,256]{5,3,4,2,1,0:T(4,128)S(1)}, f32[32,2,2,4,3,256]{5,3,4,2,1,0:T(4,128)}, u32[]{:S(2)}) copy-start(f32[32,2,2,4,3,256]{5,3,4,2,1,0:T(4,128)} %param.8) | copy-start | bytes 4718596
  3.0 48.4 %copy-start.2 = (s32[32]{0:T(128)S(1)}, s32[32]{0:T(128)}, u32[]{:S(2)}) copy-start(s32[32]{0:T(128)} %param.11) | copy-start | bytes 388
where the time goes:
time: 52.6 us; the launch traced here: 52.4 us
  Pallas kernels  48.2 us (92%)
  local copies, waits for them, and re-layouts  1.85 us (4%)
  matrix products  0.96 us (2%)
  between operations  0.72 us (1%)
  other arithmetic  0.64 us (1%)
    pallas_call x1, Pallas kernels, local_line(): lax.switch(jnp.maximum(count, 1) - 1, branches, group_of, e_view, s_view)  48.2 us
    transpose x1, local copies, waits for them, and re-layouts, local_line(): eigvecs.transpose(0, 3, 2, 1, 4).reshape(held, layers, vectors, sites)  1.69 us

commit v1 on v0

--- a/solution.py
+++ b/solution.py
@@ -8,7 +8,7 @@
 from jax.sharding import PartitionSpec as P
 
 MESH = pl.DeviceIdType.MESH
-OUT_PIECES = 4
+OUT_PIECES = 8
 PIECE_LAYERS = 1
 LANES = 128
 SUBLANES = 8
@@ -227,6 +227,13 @@
             top, rest = split(full[t, j])
             acc[t] += dot(top, high[t, j]) + (dot(top, low[t, j]) + dot(rest, high[t, j]))
 
+    layers = high.shape[1]
+
+    def contract_rows(j, at):
+        for t in range(held):
+            top, rest = split(full[t, j, at, :])
+            acc[t, at, :] += dot(top, high[t, j]) + (dot(top, low[t, j]) + dot(rest, high[t, j]))
+
     for tick in range(pieces + 3):
         i, before, late = tick, tick - 1, tick - 2
 
@@ -256,7 +263,7 @@
         last = tick - 3
         if last >= 0:
             swapped_e(last).wait_recv()
-            for layer in range(plan[last][0], sum(plan[last])):
+            for layer in range(plan[last][0], min(sum(plan[last]), layers - 1)):
                 contract(layer)
 
     for i in range(pieces):
@@ -293,8 +300,10 @@
     def back_out_o(q):
         return copy_to(give_o[q], o_recv.at[q], back_o, q, to_outer)
 
+    contract_rows(layers - 1, pl.ds(pl.multiple_of((1 - xi) * rows, rows), rows))
     for q in range(OUT_PIECES):
         x_swap(q).start()
+    contract_rows(layers - 1, pl.ds(pl.multiple_of(xi * rows, rows), rows))
 
     @pl.when(outer)
     def _():

time: 52.6 us -> 52.5 us (level)
  no operation moved by 1% of the time
where the time goes in v1:
time: 52.5 us; the launch traced here: 52.3 us
  Pallas kernels  48.1 us (92%)
  local copies, waits for them, and re-layouts  1.85 us (4%)
  matrix products  0.96 us (2%)
  between operations  0.72 us (1%)
  other arithmetic  0.64 us (1%)
    pallas_call x1, Pallas kernels, local_line(): lax.switch(jnp.maximum(count, 1) - 1, branches, group_of, e_view, s_view)  48.1 us
    transpose x1, local copies, waits for them, and re-layouts, local_line(): eigvecs.transpose(0, 3, 2, 1, 4).reshape(held, layers, vectors, sites)  1.69 us

profile of v1, /device:TPU:0, one launch (start us, length us, event | category | flops | bytes accessed | tf_op | source)
XLA Modules:
  0.0 52.3 jit_solution(15449983078273480896)
XLA Ops:
  0.0 0.0 copy-start.1
  0.0 0.0 copy-start
  0.0 1.7 %copy.12 = f32[2,3,2,128,256]{4,3,2,1,0:T(8,128)S(1)} copy(f32[2,3,2,128,256]{4,2,1,3,0:T(2,128)} %bitcast.27) | data formatting | bytes 3145728 | tf_op jit(solution)/shard_map/transpose | solution.py:359
  1.7 0.0 copy-done.1
  1.7 0.6 %fusion.3 = s32[]{:T(128)} fusion(s32[8]{0:T(128)S(1)} %copy-done.1), kind=kLoop, calls=%fused_computation.5 | loop fusion | flops 11 | bytes 20 | tf_op jit(solution)/shard_map/reduce_sum | solution.py:357
  3.0 0.0 copy-done
  3.0 0.0 copy-start.2
  3.0 48.3 %conditional.1 = (f32[2,64,2,32,4]{1,3,4,2,0:T(8,128)S(1)}) conditional(s32[]{:T(128)} %clamp.3, (s32[8]{0:T(128)S(1)}, f32[2,6,128,256]{3,2,1,0:T(8,128)S(1)}, f32[32,2,2,3,8,128]{5,4,3,2,1,0:T(8,128)S(1)}) %tuple.38, (s32[8]{0:T(128)S(1)}, f32[2,6,128,256]{3,2,1,0:T(8,128)S(1)}, ...), branch_computations={%region_1.0_spmd, %region_2.0_spmd, %region_3.0_spmd, %region_4.0_... | conditional | bytes 524296 | solution.py:403
  3.0 48.1 %project_2.1 = f32[2,64,256]{2,1,0:T(8,128)S(1)} custom-call(s32[8]{0:T(128)S(1)} %get-tuple-element.38.group_ref, f32[2,6,128,256]{3,2,1,0:T(8,128)S(1)} %get-tuple-element.39.e_ref, f32[32,2,2,3,8,128]{5,4,3,2,1,0:T(8,128)S(1)} %get-tuple-element.40.s_ref), custom_call_target="tpu_custom_call" | custom-call | tf_op jit(solution)/shard_map/cond/branch_1_fun/project_2/pallas_call | solution.py:403
  51.2 0.1 copy.9
  51.3 0.0 copy-done.2
  51.3 1.0 %convolution_bitcast_fusion = f32[2,2,4,32,64]{4,3,2,1,0:T(8,128)} fusion(f32[2,64,2,32,4]{1,3,4,2,0:T(8,128)S(1)} %get-tuple-element.47, s32[32]{0:T(128)S(1)} %broadcast_subtract_fusion), kind=kOutput, calls=%fused_computation | convolution fusion | flops 12583936 | bytes 262272 | tf_op jit(solution)/shard_map/jn,rkpns->rpsjk/dot_general | solution.py:407
  (2 shorter events, 0.0 us)
Async XLA Ops:
  0.0 1.7 %copy-start.1 = (s32[8]{0:T(128)S(1)}, s32[8]{0:T(128)}, u32[]{:S(2)}) copy-start(s32[8]{0:T(128)} %param.10) | copy-start | bytes 100
  0.0 3.0 %copy-start = (f32[32,2,2,4,3,256]{5,3,4,2,1,0:T(4,128)S(1)}, f32[32,2,2,4,3,256]{5,3,4,2,1,0:T(4,128)}, u32[]{:S(2)}) copy-start(f32[32,2,2,4,3,256]{5,3,4,2,1,0:T(4,128)} %param.8) | copy-start | bytes 4718596
  3.0 48.3 %copy-start.2 = (s32[32]{0:T(128)S(1)}, s32[32]{0:T(128)}, u32[]{:S(2)}) copy-start(s32[32]{0:T(128)} %param.11) | copy-start | bytes 388
